TPU v7x, 128 devices: a whole 4x4x4 slice. The times are simulated.
128 devices in a mesh: row: 8 (over x, core), col: 16 (over z, y).
Axes of the slice: x: 4, y: 4, z: 4, core: 2. Of those that a mesh axis runs over, the one named last changes fastest.
Arguments:
- matrix: float32 [8192, 8192], P('row', 'col'), as said below
- start_vectors: float32 [8192, 512], P(('col', 'row')), may hold values from -6 to 6
- interval: float32 [2], replicated, as said below
Outputs:
- ortho_basis: float32 [8192, 512], P(('col', 'row'))
- projected: float32 [512, 512], replicated
- residual: float32 [8192, 512], P(('col', 'row'))
Inputs may be any that keep to these rules, and one draw needn't show every extreme that they name: matrix is exactly symmetric (entry (r, c) equals entry (c, r)); its eigenvalues lie within about -1.45 to 1.45. interval[0] lies in [-1.2, -0.7] and interval[1] in [1.45, 1.9].
All inputs are finite; a program needn't handle non-finite values.
Results may differ from a plain program's by a relative error of at most 0.0003.
Values sent between devices are 32-bit elements.
A program may use at most 128 MiB of HBM per device.

v0:
```python
import jax
import jax.numpy as jnp
from jax import lax
from jax.experimental import pallas as pl
from jax.experimental.pallas import tpu as pltpu
from jax.sharding import Mesh
from jax.sharding import PartitionSpec as P

ROW = ("row_0", "row_1")
COL = ("col_0", "col_1")
COL_ROW = ("col_0", "col_1", "row_0", "row_1")
MESH = pl.DeviceIdType.MESH
F32 = jnp.float32
BF16 = jnp.bfloat16
AXES6 = ("xa", "xb", "ya", "yb", "za", "zb"), ("xb", "xa", "yb", "ya", "zb", "za")
SUM_LINKS = tuple(order[k:] + order[:k] for k in (0, 2, 4) for order in AXES6)
SUM_HALF = 48, 48, 40, 40, 40, 40
SUM_START = 0, 96, 192, 272, 352, 432
VMEM_LIMIT = 63 * 1024 * 1024
LINKS = ("ya", "yb", "za", "zb"), ("yb", "ya", "zb", "za"), ("za", "zb", "ya", "yb"), ("zb", "za", "yb", "ya")


class Place:
    def __init__(self):
        self.x = lax.axis_index("row_0")
        self.core = lax.axis_index("row_1")
        self.z = lax.axis_index("col_0")
        self.y = lax.axis_index("col_1")
        self.at = {"x": self.x, "y": self.y, "z": self.z}

    def device(self, x=None, core=None, z=None, y=None):
        pick = lambda given, own: own if given is None else given
        return (pick(x, self.x), pick(core, self.core), pick(z, self.z), pick(y, self.y))

    def sibling(self):
        return self.device(core=1 - self.core)

    def partner(self, link):
        v = self.at[link[0]]
        w = v + 1 - 2 * (v % 2) if link[1] == "a" else 3 - v
        return self.device(**{link[0]: w})

    def bit(self, link):
        v = self.at[link[0]]
        return ((v + 1) // 2) % 2 if link[1] == "a" else v // 2


def remote(src, dst, send, recv, device):
    return pltpu.make_async_remote_copy(
        src_ref=src, dst_ref=dst, send_sem=send, recv_sem=recv, device_id=device, device_id_type=MESH
    )


def rows_at(start, size):
    return pl.ds(pl.multiple_of(start, size), size)


def chosen(index, values):
    result = values[-1]
    for i, value in list(enumerate(values))[-2::-1]:
        result = jnp.where(index == i, value, result)
    return result


def lanes_at(start, size):
    return pl.ds(pl.multiple_of(start, 128), size)


def halves(value):
    hi = value.astype(BF16)
    return hi, (value - hi.astype(F32)).astype(BF16)


def dot(left, right):
    return jnp.dot(left, right, preferred_element_type=F32)


def thirds(value):
    a = value.astype(BF16)
    rest = value - a.astype(F32)
    b = rest.astype(BF16)
    return a, b, (rest - b.astype(F32)).astype(BF16)


def small_factor(tile):
    sub = lax.broadcasted_iota(jnp.int32, (8, 128), 0)
    w = [tile[8 * i : 8 * i + 8, :] for i in range(8)]
    for p in range(8):
        col = {(i, c): jnp.broadcast_to(w[i][:, 8 * p + c : 8 * p + c + 1], (8, 128)) for i in range(p, 8) for c in range(8)}
        for c in range(8):
            inv = lax.rsqrt(jnp.broadcast_to(col[p, c][c : c + 1, :], (8, 128)))
            row = jnp.broadcast_to(w[p][c : c + 1, :], (8, 128)) * inv
            own = col[p, c] * inv
            below = sub > c
            w[p] = jnp.where(below, w[p] - own * row, jnp.where(sub == c, row, w[p]))
            steps = [jnp.broadcast_to(col[p, c][d : d + 1, :], (8, 128)) * inv for d in range(c + 1, 8)]
            for d in range(c + 1, 8):
                col[p, d] = col[p, d] - own * steps[d - c - 1]
            for i in range(p + 1, 8):
                mult = col[i, c] * inv
                w[i] = w[i] - mult * row
                for d in range(c + 1, 8):
                    col[i, d] = col[i, d] - mult * steps[d - c - 1]
    return jnp.concatenate(w, axis=0)


def factor_blocks(x, first, last):
    def block(k, carry):
        here = pl.ds(pl.multiple_of(64 * k, 64), 64)
        pair = pl.ds(pl.multiple_of(128 * (k // 2), 128), 128)
        odd = k % 2
        lane = lax.broadcasted_iota(jnp.int32, (64, 128), 1)
        rowi = lax.broadcasted_iota(jnp.int32, (64, 128), 0)
        a = x[here, pair]
        a = jnp.where(odd == 1, pltpu.roll(a, 64, 1), a)
        w = small_factor(jnp.where(lane < 64, a, (lane - 64 == rowi).astype(F32)))
        linv = pltpu.roll(w, 64, 1)[:, :64]
        rows = jnp.dot(linv, x[here, :], precision=lax.Precision.HIGHEST, preferred_element_type=F32)
        x[here, :] = rows
        placed = jnp.where(odd == 1, w, pltpu.roll(w, 64, 1))
        x[here, pair] = jnp.where(lane // 64 == odd, placed, x[here, pair])
        full = x[here, :]
        wide = lax.broadcasted_iota(jnp.int32, (64, 512), 1)
        left = jnp.where(wide // 64 > k, full, 0.0)
        h, m, l = thirds(full)
        lh, lm, ll = thirds(left)
        right = jnp.concatenate([h, m, h, m, l, h], axis=0)
        lefts = jnp.concatenate([lh, lh, lm, lm, lh, ll], axis=0)
        update = lax.dot_general(lefts, right, (((0,), (0,)), ((), ())), preferred_element_type=F32)
        r = lax.broadcasted_iota(jnp.int32, (512, 512), 0)
        c = lax.broadcasted_iota(jnp.int32, (512, 512), 1)
        x[...] = jnp.where((c // 64 == k) & (r // 64 > k), 0.0, x[...]) - update
        return carry

    lax.fori_loop(first, last, block, 0)


def lower_only(x):
    for i in range(4):
        strip = pl.ds(128 * i, 128)
        r = 128 * i + lax.broadcasted_iota(jnp.int32, (128, 512), 0)
        c = lax.broadcasted_iota(jnp.int32, (128, 512), 1)
        x[strip, :] = jnp.where(c <= r, x[strip, :], 0.0)


def precise(lefts, rights):
    (a, b, c), (x, y, z) = lefts, rights
    return (dot(b, y) + dot(a, z) + dot(c, x)) + (dot(a, y) + dot(b, x)) + dot(a, x)


def precise_gram(lefts, rights):
    (a, b, c), (x, y, z) = lefts, rights
    tall = jnp.concatenate([a, a, b, b, a, c], axis=0)
    other = jnp.concatenate([x, y, x, y, z, x], axis=0)
    return lax.dot_general(tall, other, (((0,), (0,)), ((), ())), preferred_element_type=F32)


def chain_kernel(
    interval, matrix, slab, basis_out, proj_out, resid_out,
    other, m_hi, m_lo, t_hi, t_lo, cols, rows, part, split_c, split_r,
    r1, h1, r2, h2, r3, h3, r4, share,
    tb, rb1, tb2, rb2, full, mapped, local, total, term, got, inverse, cross, turned, parts,
    f_send, f_recv, b_send, b_recv, g_send, g_recv, m_send, m_recv, p_send, p_recv, s_send, s_recv,
    a_send, a_recv, x_send, x_recv,
):
    me = Place()
    block = me.z * 4 + me.y

    barrier = pltpu.get_barrier_semaphore()
    near = [me.device(x=(me.x + d // 2) % 4, core=(me.core + d) % 2) for d in range(1, 8)]
    near += [me.partner(link) for link in ("ya", "yb", "za", "zb")]
    for device in near:
        pl.semaphore_signal(barrier, inc=1, device_id=device, device_id_type=MESH)
    pl.semaphore_wait(barrier, len(near))

    swap = remote(matrix, other, m_send, m_recv, me.sibling())
    swap.start()

    def slab_rows(x, core):
        return rows_at((x * 2 + core) * 64, 64)

    gathers = []
    for d in range(1, 8):
        to_x, to_core = (me.x + d // 2) % 4, (me.core + d) % 2
        for c in range(2):
            copy = remote(
                slab.at[:, lanes_at(256 * to_core + 128 * c, 128)], cols.at[0, c, slab_rows(me.x, me.core)],
                g_send.at[d, c], g_recv.at[d, c], me.device(x=to_x, core=to_core),
            )
            copy.start()
            gathers.append((d, c, copy))
    for c in range(2):
        cols[0, c, slab_rows(me.x, me.core), :] = slab[:, lanes_at(256 * me.core + 128 * c, 128)]

    center = 0.5 * (interval[0] + interval[1])
    half_width = 0.5 * (interval[1] - interval[0])

    def prepare(source, half):
        def tile(i, carry):
            base = half * 1024 + i * 256
            value = source[rows_at(i * 256, 256), :]
            row = me.x * 2048 + base + lax.broadcasted_iota(jnp.int32, (256, 512), 0)
            col = block * 512 + lax.broadcasted_iota(jnp.int32, (256, 512), 1)
            value = jnp.where(row == col, value - center, value) / half_width
            hi, lo = halves(value)
            where = rows_at(base, 256)
            m_hi[where, :] = hi
            m_lo[where, :] = lo
            hi, lo = halves(value.T)
            t_hi[:, where] = hi
            t_lo[:, where] = lo
            return carry

        lax.fori_loop(0, 4, tile, 0)

    prepare(matrix, me.core)
    swap.wait()
    prepare(other, 1 - me.core)
    for d, c, copy in gathers:
        copy.wait()

    def forward(c, f, source, target, before, last=False):
        hi, lo = halves(cols[source, c])
        split_c[c, :, :128] = hi
        split_c[c, :, 128:] = lo
        copies = {}

        def send(q, step, src, dst, link):
            copies[q, step] = remote(src, dst, f_send.at[f, c, q, step], f_recv.at[f, c, q, step], me.partner(link))
            copies[q, step].start()

        links = [order[0] for order in LINKS]

        def multiply(q, carry):
            strip = rows_at(512 * q, 512)
            both = split_c[c]
            product = dot(m_hi[strip, :], both) + dot(m_lo[strip, :], both)
            part[c, strip, :] = product[:, :128] + product[:, 128:]
            k1 = chosen(q, [me.bit(link) for link in links])
            there = [chosen(q, [me.partner(link)[i] for link in links]) for i in range(4)]
            remote(
                part.at[c, rows_at(512 * q + 256 * (1 - k1), 256)], r1.at[f, c, q],
                f_send.at[f, c, q, 0], f_recv.at[f, c, q, 0], tuple(there),
            ).start()
            return carry

        lax.fori_loop(0, 4, multiply, 0)
        where1, where2 = [], []
        for q, (l1, l2, l3, l4) in enumerate(LINKS):
            k1, k2 = me.bit(l1), me.bit(l2)
            where1.append(512 * q + 256 * k1)
            where2.append(512 * q + 256 * k1 + 128 * k2)
            copies[q, 0] = remote(
                part.at[c, rows_at(512 * q + 256 * (1 - k1), 256)], r1.at[f, c, q],
                f_send.at[f, c, q, 0], f_recv.at[f, c, q, 0], me.partner(l1),
            )
        yield
        for q, (l1, l2, l3, l4) in enumerate(LINKS):
            k2 = me.bit(l2)
            copies[q, 0].wait_recv()
            h1[c, q] = part[c, rows_at(where1[q], 256), :] + r1[f, c, q]
            send(q, 1, h1.at[c, q, rows_at(128 * (1 - k2), 128)], r2.at[f, c, q], l2)
        yield
        for q, (l1, l2, l3, l4) in enumerate(LINKS):
            k2 = me.bit(l2)
            copies[q, 1].wait_recv()
            h2[c, q] = h1[c, q, rows_at(128 * k2, 128), :] + r2[f, c, q]
            if not last:
                send(q, 2, h2.at[c, q], r3.at[f, c, q], l3)
        if last:
            for copy in copies.values():
                copy.wait_send()
            return
        yield
        for q, (l1, l2, l3, l4) in enumerate(LINKS):
            copies[q, 2].wait_recv()
            h3[c, q] = h2[c, q] + r3[f, c, q]
            send(q, 3, h3.at[c, q], r4.at[f, c, q], l4)
        yield
        for q, (l1, l2, l3, l4) in enumerate(LINKS):
            copies[q, 3].wait_recv()
            total = h3[c, q] + r4[f, c, q]
            here = rows_at(where2[q], 128)
            if before is not None:
                total = 2.0 * total - rows[before, c, here, :]
            rows[target, c, here, :] = total
            send(q, 4, rows.at[target, c, here], rows.at[target, c, here], l2)
        yield
        for q, (l1, l2, l3, l4) in enumerate(LINKS):
            copies[q, 4].wait_recv()
            here = rows_at(where1[q], 256)
            send(q, 5, rows.at[target, c, here], rows.at[target, c, here], l1)
        yield
        for q in range(4):
            copies[q, 5].wait_recv()
        for copy in copies.values():
            copy.wait_send()

    def backward(c, b, source, target, before):
        def split(i, carry):
            strip = rows_at(512 * i, 512)
            hi, lo = halves(rows[source, c, strip, :])
            split_r[c, strip, :128] = hi
            split_r[c, strip, 128:] = lo
            return carry

        lax.fori_loop(0, 4, split, 0)
        orders = ("xa", "xb"), ("xb", "xa")
        copies = {}

        def send(s, step, src, dst, link):
            copies[s, step] = remote(src, dst, b_send.at[b, c, s, step], b_recv.at[b, c, s, step], me.partner(link))
            copies[s, step].start()

        def multiply(s, carry):
            strip = rows_at(256 * s, 256)
            both = split_r[c]
            product = dot(t_hi[strip, :], both) + dot(t_lo[strip, :], both)
            tb[c, strip, :] = product[:, :128] + product[:, 128:]
            there = [chosen(s, [me.partner(order[0])[i] for order in orders]) for i in range(4)]
            remote(
                tb.at[c, strip], rb1.at[b, c, strip], b_send.at[b, c, s, 0], b_recv.at[b, c, s, 0], tuple(there)
            ).start()
            return carry

        lax.fori_loop(0, 2, multiply, 0)
        for s in range(2):
            strip = pl.ds(256 * s, 256)
            copies[s, 0] = remote(
                tb.at[c, strip], rb1.at[b, c, strip],
                b_send.at[b, c, s, 0], b_recv.at[b, c, s, 0], me.partner(orders[s][0]),
            )
        yield
        for s in range(2):
            strip = pl.ds(256 * s, 256)
            copies[s, 0].wait_recv()
            tb2[c, strip, :] = tb[c, strip, :] + rb1[b, c, strip, :]
            send(s, 1, tb2.at[c, strip], rb2.at[b, c, strip], orders[s][1])
        yield
        for s in range(2):
            strip = pl.ds(256 * s, 256)
            copies[s, 1].wait_recv()
            total = tb2[c, strip, :] + rb2[b, c, strip, :]
            if before is not None:
                total = 2.0 * total - cols[before, c, strip, :]
            cols[target, c, strip, :] = total
        for copy in copies.values():
            copy.wait_send()

    done = set()

    def chain(c):
        yield from forward(c, 0, 0, 0, None)
        yield from backward(c, 0, 0, 1, 0)
        yield from forward(c, 1, 1, 1, 0)
        done.add(("y3", c))
        yield from backward(c, 1, 1, 2, None)
        yield from forward(c, 2, 2, 2, 1)
        yield from backward(c, 2, 2, 3, 2)
        done.add(("v3", c))
        yield from forward(c, 3, 3, None, None, last=True)
        mine = lanes_at(256 * me.core + 128 * c, 128)
        pending = []
        own_index = None
        for q, (l1, l2, l3, l4) in enumerate(LINKS):
            k1, k2, k3, k4 = me.bit(l1), me.bit(l2), me.bit(l3), me.bit(l4)
            to_x, to_y, to_z = 2 * k1 + k2, q, me.x
            index = 2 * k3 + k4
            same = (to_x == me.x) & (to_y == me.y) & (to_z == me.z)
            own_index = jnp.where(same, index, -1 if own_index is None else own_index)
            copy = remote(
                h2.at[c, q], share.at[c, index],
                p_send.at[c, q], p_recv.at[c, index], me.device(x=to_x, y=to_y, z=to_z),
            )

            @pl.when(jnp.logical_not(same))
            def _():
                copy.start()

            @pl.when(same)
            def _():
                share[c, index] = h2[c, q]

            pending.append((same, copy))
        yield
        for same, copy in pending:

            @pl.when(jnp.logical_not(same))
            def _():
                copy.wait_send()

        for index in range(4):

            @pl.when(own_index != index)
            def _():
                remote(
                    h2.at[c, 0], share.at[c, index], p_send.at[c, 0], p_recv.at[c, index], me.sibling()
                ).wait_recv()

        full[2, :, mine] = (share[c, 0] + share[c, 1]) + (share[c, 2] + share[c, 3])
        done.add(("z2", c))

    half = lanes_at(256 * me.core, 256)

    def needs(*marks):
        while not all(mark in done for mark in marks):
            yield "blocked"

    def swap_slab(k):
        copy = remote(full.at[k, :, half], full.at[k, :, half], s_send.at[k], s_recv.at[k], me.sibling())
        copy.start()
        yield
        copy.wait()

    def all_sum(n, target):
        copies = {}

        def send(s, t, src, dst, link):
            copies[s, t] = remote(src, dst, a_send.at[n, s, t], a_recv.at[n, s, t], me.partner(link))
            copies[s, t].start()

        def piece(s, k):
            return pl.ds(pl.multiple_of(SUM_START[s] + SUM_HALF[s] * k, 8), SUM_HALF[s])

        for s, order in enumerate(SUM_LINKS):
            small = pl.ds(0, SUM_HALF[s])
            send(s, 0, local.at[n, piece(s, 1 - me.bit(order[0]))], got.at[n, 0, s, small], order[0])
        yield
        for t in range(1, 6):
            for s, order in enumerate(SUM_LINKS):
                small = pl.ds(0, SUM_HALF[s])
                copies[s, t - 1].wait_recv()
                before = local[n, piece(s, me.bit(order[0])), :] if t == 1 else term[n % 2, t - 2, s, small, :]
                term[n % 2, t - 1, s, small, :] = before + got[n, t - 1, s, small, :]
                send(s, t, term.at[n % 2, t - 1, s, small], got.at[n, t, s, small], order[t])
            yield
        for s, order in enumerate(SUM_LINKS):
            small = pl.ds(0, SUM_HALF[s])
            copies[s, 5].wait_recv()
            here = piece(s, me.bit(order[0]))
            total[n, here, :] = term[n % 2, 4, s, small, :] + got[n, 5, s, small, :]
            send(s, 6, total.at[n, here], total.at[n, here], order[0])
        yield
        for s in range(6):
            copies[s, 6].wait_recv()
        copy = remote(total.at[n], target.at[:, half], x_send.at[n], x_recv.at[n], me.sibling())
        copy.start()
        target[:, half] = total[n]
        for one in copies.values():
            one.wait_send()
        yield
        copy.wait()

    def keep_transposed(x):
        for i, one in enumerate(thirds(x[...].T)):
            turned[i] = one

    def transposed():
        return turned[0], turned[1], turned[2]

    def first_factor():
        yield from needs(("y3", 0), ("y3", 1))
        for c in range(2):
            full[0, :, lanes_at(256 * me.core + 128 * c, 128)] = rows[1, c, rows_at(block * 128, 128), :]
        yield from swap_slab(0)
        local[0] = precise_gram(thirds(full[0]), thirds(full[0, :, half])) / 8192
        yield from all_sum(0, inverse.at[0])
        for k in range(0, 8, 2):
            factor_blocks(inverse.at[0], k, k + 2)
            yield
        lower_only(inverse.at[0])
        keep_transposed(inverse.at[0])
        done.add("first")

    def second_factor():
        yield from needs(("v3", 0), ("v3", 1))
        for c in range(2):
            full[1, :, lanes_at(256 * me.core + 128 * c, 128)] = cols[3, c, rows_at(me.x * 128, 128), :]
        yield from swap_slab(1)
        yield from needs("first")
        mapped[0] = precise(thirds(full[1]), transposed())
        local[1] = precise_gram(thirds(mapped[0]), thirds(mapped[0, :, half])) / 8192
        done.add("filtered")
        yield from all_sum(1, inverse.at[1])
        for k in range(0, 8, 2):
            factor_blocks(inverse.at[1], k, k + 2)
            yield
        lower_only(inverse.at[1])
        done.add("second")

    def cross_terms():
        yield from needs(("z2", 0), ("z2", 1), "filtered")
        yield from swap_slab(2)
        mapped[1] = precise(thirds(full[2]), transposed())
        local[2] = precise_gram(thirds(mapped[0]), thirds(mapped[1, :, half])) / 8192
        yield from all_sum(2, cross)

    live = [chain(0), chain(1), first_factor(), second_factor(), cross_terms()]
    while live:
        for one in list(live):
            if next(one, "end") == "end":
                live.remove(one)

    keep_transposed(inverse.at[1])
    mine = rows_at(64 * me.core, 64)
    basis = precise(thirds(mapped[0, mine, :]), transposed())
    basis_out[...] = basis
    for i, one in enumerate(thirds(cross[...])):
        parts[i] = one

    def solve_left(i, carry):
        strip = rows_at(256 * i, 256)
        cross[strip, :] = precise(thirds(inverse[1, strip, :]), (parts[0], parts[1], parts[2]))
        return carry

    lax.fori_loop(0, 2, solve_left, 0)

    def solve_right(i, carry):
        strip = rows_at(256 * i, 256)
        proj_out[strip, :] = precise(thirds(cross[strip, :]), transposed())
        return carry

    lax.fori_loop(0, 2, solve_right, 0)
    rest = mapped[1, mine, :] - precise(thirds(basis), thirds(cross[...]))
    resid_out[...] = precise(thirds(rest), transposed())


def chain_call(matrix, slab, interval):
    vm = pl.BlockSpec(memory_space=pltpu.VMEM)
    dma = pltpu.SemaphoreType.DMA
    slab_shape = jax.ShapeDtypeStruct((64, 512), F32)
    return pl.pallas_call(
        chain_kernel,
        out_shape=(slab_shape, jax.ShapeDtypeStruct((512, 512), F32), slab_shape),
        in_specs=[pl.BlockSpec(memory_space=pltpu.SMEM), vm, vm],
        out_specs=(vm, vm, vm),
        scratch_shapes=[
            pltpu.VMEM((1024, 512), F32),
            pltpu.VMEM((2048, 512), BF16),
            pltpu.VMEM((2048, 512), BF16),
            pltpu.VMEM((512, 2048), BF16),
            pltpu.VMEM((512, 2048), BF16),
            pltpu.VMEM((4, 2, 512, 128), F32),
            pltpu.VMEM((3, 2, 2048, 128), F32),
            pltpu.VMEM((2, 2048, 128), F32),
            pltpu.VMEM((2, 512, 256), BF16),
            pltpu.VMEM((2, 2048, 256), BF16),
            pltpu.VMEM((4, 2, 4, 256, 128), F32),
            pltpu.VMEM((2, 4, 256, 128), F32),
            pltpu.VMEM((4, 2, 4, 128, 128), F32),
            pltpu.VMEM((2, 4, 128, 128), F32),
            pltpu.VMEM((3, 2, 4, 128, 128), F32),
            pltpu.VMEM((2, 4, 128, 128), F32),
            pltpu.VMEM((3, 2, 4, 128, 128), F32),
            pltpu.VMEM((2, 4, 128, 128), F32),
            pltpu.VMEM((2, 512, 128), F32),
            pltpu.VMEM((3, 2, 512, 128), F32),
            pltpu.VMEM((2, 512, 128), F32),
            pltpu.VMEM((3, 2, 512, 128), F32),
            pltpu.VMEM((3, 128, 512), F32),
            pltpu.VMEM((2, 128, 512), F32),
            pltpu.VMEM((3, 512, 256), F32),
            pltpu.VMEM((3, 512, 256), F32),
            pltpu.VMEM((2, 5, 6, 48, 256), F32),
            pltpu.VMEM((3, 6, 6, 48, 256), F32),
            pltpu.VMEM((2, 512, 512), F32),
            pltpu.VMEM((512, 512), F32),
            pltpu.VMEM((3, 512, 512), BF16),
            pltpu.VMEM((3, 512, 512), BF16),
            dma((4, 2, 4, 6)),
            dma((4, 2, 4, 6)),
            dma((3, 2, 2, 2)),
            dma((3, 2, 2, 2)),
            dma((8, 2)),
            dma((8, 2)),
            dma,
            dma,
            dma((2, 4)),
            dma((2, 4)),
            dma((3,)),
            dma((3,)),
            dma((3, 6, 7)),
            dma((3, 6, 7)),
            dma((3,)),
            dma((3,)),
        ],
        compiler_params=pltpu.CompilerParams(has_side_effects=True, collective_id=0, vmem_limit_bytes=VMEM_LIMIT),
    )(interval, matrix, slab)


def shards(matrix, start_vectors, interval):
    return chain_call(matrix, start_vectors, interval)


def solution(mesh):
    torus = Mesh(mesh.devices.reshape(4, 2, 4, 4), ("row_0", "row_1", "col_0", "col_1"))
    placed = (P(ROW, COL), P(COL_ROW, None), P())
    return jax.shard_map(
        shards,
        mesh=torus,
        in_specs=placed,
        out_specs=(P(COL_ROW, None), P(), P(COL_ROW, None)),
        check_vma=False,
    )
```

profile of v0, /device:TPU:1, one launch (start us, length us, event | category | flops | bytes accessed | tf_op | source)
XLA Modules:
  0.0 246.9 jit_solution(16040142791980834060)
XLA Ops:
  0.6 241.7 %shard_map.58 = (f32[64,512]{1,0:T(8,128)}, f32[512,512]{1,0:T(8,128)}, f32[64,512]{1,0:T(8,128)}) custom-call(f32[2]{0:T(128)} %interval.1, f32[1024,512]{1,0:T(8,128)} %matrix.1, f32[64,512]{1,0:T(8,128)} %slab.1), custom_call_target="tpu_custom_call" | custom-call | tf_op jit(solution)/shard_map/pallas_call | solution.py:532
  242.4 0.0 copy-start
  242.4 1.6 copy.9
  244.0 2.3 copy.10
  246.3 0.0 copy-done
  246.3 0.7 copy.11
Async XLA Ops:
  242.4 3.9 %copy-start = (f32[64,512]{1,0:T(8,128)S(1)}, f32[64,512]{1,0:T(8,128)}, u32[]{:S(2)}) copy-start(f32[64,512]{1,0:T(8,128)} %get-tuple-element.8) | copy-start | bytes 393220
where the time goes:
time: 247 us
  Pallas kernels  242 us (98%)
  local copies, waits for them, and re-layouts  4.52 us (2%)
    pallas_call x1, Pallas kernels, chain_call(): pl.pallas_call(chain_kernel, out_shape=(slab_shape, jax.ShapeDtypeStruct(...  242 us

commit v1 on v0

--- a/solution.py
+++ b/solution.py
@@ -18,6 +18,7 @@
 SUM_START = 0, 96, 192, 272, 352, 432
 VMEM_LIMIT = 63 * 1024 * 1024
 LINKS = ("ya", "yb", "za", "zb"), ("yb", "ya", "zb", "za"), ("za", "zb", "ya", "yb"), ("zb", "za", "yb", "ya")
+STREAMS = LINKS + LINKS
 
 
 class Place:
@@ -104,35 +105,31 @@
     return jnp.concatenate(w, axis=0)
 
 
-def factor_blocks(x, first, last):
-    def block(k, carry):
-        here = pl.ds(pl.multiple_of(64 * k, 64), 64)
-        pair = pl.ds(pl.multiple_of(128 * (k // 2), 128), 128)
-        odd = k % 2
-        lane = lax.broadcasted_iota(jnp.int32, (64, 128), 1)
-        rowi = lax.broadcasted_iota(jnp.int32, (64, 128), 0)
-        a = x[here, pair]
-        a = jnp.where(odd == 1, pltpu.roll(a, 64, 1), a)
-        w = small_factor(jnp.where(lane < 64, a, (lane - 64 == rowi).astype(F32)))
-        linv = pltpu.roll(w, 64, 1)[:, :64]
-        rows = jnp.dot(linv, x[here, :], precision=lax.Precision.HIGHEST, preferred_element_type=F32)
-        x[here, :] = rows
-        placed = jnp.where(odd == 1, w, pltpu.roll(w, 64, 1))
-        x[here, pair] = jnp.where(lane // 64 == odd, placed, x[here, pair])
-        full = x[here, :]
-        wide = lax.broadcasted_iota(jnp.int32, (64, 512), 1)
-        left = jnp.where(wide // 64 > k, full, 0.0)
-        h, m, l = thirds(full)
-        lh, lm, ll = thirds(left)
-        right = jnp.concatenate([h, m, h, m, l, h], axis=0)
-        lefts = jnp.concatenate([lh, lh, lm, lm, lh, ll], axis=0)
-        update = lax.dot_general(lefts, right, (((0,), (0,)), ((), ())), preferred_element_type=F32)
-        r = lax.broadcasted_iota(jnp.int32, (512, 512), 0)
-        c = lax.broadcasted_iota(jnp.int32, (512, 512), 1)
-        x[...] = jnp.where((c // 64 == k) & (r // 64 > k), 0.0, x[...]) - update
-        return carry
-
-    lax.fori_loop(first, last, block, 0)
+def factor_block(x, k):
+    here = pl.ds(pl.multiple_of(64 * k, 64), 64)
+    pair = pl.ds(pl.multiple_of(128 * (k // 2), 128), 128)
+    odd = k % 2
+    lane = lax.broadcasted_iota(jnp.int32, (64, 128), 1)
+    rowi = lax.broadcasted_iota(jnp.int32, (64, 128), 0)
+    a = x[here, pair]
+    a = jnp.where(odd == 1, pltpu.roll(a, 64, 1), a)
+    w = small_factor(jnp.where(lane < 64, a, (lane - 64 == rowi).astype(F32)))
+    linv = pltpu.roll(w, 64, 1)[:, :64]
+    rows = jnp.dot(linv, x[here, :], precision=lax.Precision.HIGHEST, preferred_element_type=F32)
+    x[here, :] = rows
+    placed = jnp.where(odd == 1, w, pltpu.roll(w, 64, 1))
+    x[here, pair] = jnp.where(lane // 64 == odd, placed, x[here, pair])
+    full = x[here, :]
+    wide = lax.broadcasted_iota(jnp.int32, (64, 512), 1)
+    left = jnp.where(wide // 64 > k, full, 0.0)
+    h, m, l = thirds(full)
+    lh, lm, ll = thirds(left)
+    right = jnp.concatenate([h, m, h, m, l, h], axis=0)
+    lefts = jnp.concatenate([lh, lh, lm, lm, lh, ll], axis=0)
+    update = lax.dot_general(lefts, right, (((0,), (0,)), ((), ())), preferred_element_type=F32)
+    r = lax.broadcasted_iota(jnp.int32, (512, 512), 0)
+    c = lax.broadcasted_iota(jnp.int32, (512, 512), 1)
+    x[...] = jnp.where((c // 64 == k) & (r // 64 > k), 0.0, x[...]) - update
 
 
 def lower_only(x):
@@ -229,42 +226,42 @@
             copies[q, step] = remote(src, dst, f_send.at[f, c, q, step], f_recv.at[f, c, q, step], me.partner(link))
             copies[q, step].start()
 
-        links = [order[0] for order in LINKS]
-
         def multiply(q, carry):
             strip = rows_at(512 * q, 512)
             both = split_c[c]
             product = dot(m_hi[strip, :], both) + dot(m_lo[strip, :], both)
             part[c, strip, :] = product[:, :128] + product[:, 128:]
-            k1 = chosen(q, [me.bit(link) for link in links])
-            there = [chosen(q, [me.partner(link)[i] for link in links]) for i in range(4)]
-            remote(
-                part.at[c, rows_at(512 * q + 256 * (1 - k1), 256)], r1.at[f, c, q],
-                f_send.at[f, c, q, 0], f_recv.at[f, c, q, 0], tuple(there),
-            ).start()
+            for u in range(2):
+                links = [STREAMS[2 * i + u][0] for i in range(4)]
+                k1 = chosen(q, [me.bit(link) for link in links])
+                there = [chosen(q, [me.partner(link)[i] for link in links]) for i in range(4)]
+                remote(
+                    part.at[c, rows_at(512 * q + 256 * u + 128 * (1 - k1), 128)], r1.at[f, c, 2 * q + u],
+                    f_send.at[f, c, 2 * q + u, 0], f_recv.at[f, c, 2 * q + u, 0], tuple(there),
+                ).start()
             return carry
 
         lax.fori_loop(0, 4, multiply, 0)
         where1, where2 = [], []
-        for q, (l1, l2, l3, l4) in enumerate(LINKS):
+        for q, (l1, l2, l3, l4) in enumerate(STREAMS):
             k1, k2 = me.bit(l1), me.bit(l2)
-            where1.append(512 * q + 256 * k1)
-            where2.append(512 * q + 256 * k1 + 128 * k2)
+            where1.append(256 * q + 128 * k1)
+            where2.append(256 * q + 128 * k1 + 64 * k2)
             copies[q, 0] = remote(
-                part.at[c, rows_at(512 * q + 256 * (1 - k1), 256)], r1.at[f, c, q],
+                part.at[c, rows_at(256 * q + 128 * (1 - k1), 128)], r1.at[f, c, q],
                 f_send.at[f, c, q, 0], f_recv.at[f, c, q, 0], me.partner(l1),
             )
         yield
-        for q, (l1, l2, l3, l4) in enumerate(LINKS):
+        for q, (l1, l2, l3, l4) in enumerate(STREAMS):
             k2 = me.bit(l2)
             copies[q, 0].wait_recv()
-            h1[c, q] = part[c, rows_at(where1[q], 256), :] + r1[f, c, q]
-            send(q, 1, h1.at[c, q, rows_at(128 * (1 - k2), 128)], r2.at[f, c, q], l2)
-        yield
-        for q, (l1, l2, l3, l4) in enumerate(LINKS):
+            h1[c, q] = part[c, rows_at(where1[q], 128), :] + r1[f, c, q]
+            send(q, 1, h1.at[c, q, rows_at(64 * (1 - k2), 64)], r2.at[f, c, q], l2)
+        yield
+        for q, (l1, l2, l3, l4) in enumerate(STREAMS):
             k2 = me.bit(l2)
             copies[q, 1].wait_recv()
-            h2[c, q] = h1[c, q, rows_at(128 * k2, 128), :] + r2[f, c, q]
+            h2[c, q] = h1[c, q, rows_at(64 * k2, 64), :] + r2[f, c, q]
             if not last:
                 send(q, 2, h2.at[c, q], r3.at[f, c, q], l3)
         if last:
@@ -272,26 +269,26 @@
                 copy.wait_send()
             return
         yield
-        for q, (l1, l2, l3, l4) in enumerate(LINKS):
+        for q, (l1, l2, l3, l4) in enumerate(STREAMS):
             copies[q, 2].wait_recv()
             h3[c, q] = h2[c, q] + r3[f, c, q]
             send(q, 3, h3.at[c, q], r4.at[f, c, q], l4)
         yield
-        for q, (l1, l2, l3, l4) in enumerate(LINKS):
+        for q, (l1, l2, l3, l4) in enumerate(STREAMS):
             copies[q, 3].wait_recv()
             total = h3[c, q] + r4[f, c, q]
-            here = rows_at(where2[q], 128)
+            here = rows_at(where2[q], 64)
             if before is not None:
                 total = 2.0 * total - rows[before, c, here, :]
             rows[target, c, here, :] = total
             send(q, 4, rows.at[target, c, here], rows.at[target, c, here], l2)
         yield
-        for q, (l1, l2, l3, l4) in enumerate(LINKS):
+        for q, (l1, l2, l3, l4) in enumerate(STREAMS):
             copies[q, 4].wait_recv()
-            here = rows_at(where1[q], 256)
+            here = rows_at(where1[q], 128)
             send(q, 5, rows.at[target, c, here], rows.at[target, c, here], l1)
         yield
-        for q in range(4):
+        for q in range(8):
             copies[q, 5].wait_recv()
         for copy in copies.values():
             copy.wait_send()
@@ -317,28 +314,30 @@
             both = split_r[c]
             product = dot(t_hi[strip, :], both) + dot(t_lo[strip, :], both)
             tb[c, strip, :] = product[:, :128] + product[:, 128:]
-            there = [chosen(s, [me.partner(order[0])[i] for order in orders]) for i in range(4)]
-            remote(
-                tb.at[c, strip], rb1.at[b, c, strip], b_send.at[b, c, s, 0], b_recv.at[b, c, s, 0], tuple(there)
-            ).start()
+            for u in range(2):
+                strip = rows_at(256 * s + 128 * u, 128)
+                remote(
+                    tb.at[c, strip], rb1.at[b, c, strip],
+                    b_send.at[b, c, 2 * s + u, 0], b_recv.at[b, c, 2 * s + u, 0], me.partner(orders[u][0]),
+                ).start()
             return carry
 
         lax.fori_loop(0, 2, multiply, 0)
-        for s in range(2):
-            strip = pl.ds(256 * s, 256)
+        for s in range(4):
+            strip = pl.ds(128 * s, 128)
             copies[s, 0] = remote(
                 tb.at[c, strip], rb1.at[b, c, strip],
-                b_send.at[b, c, s, 0], b_recv.at[b, c, s, 0], me.partner(orders[s][0]),
+                b_send.at[b, c, s, 0], b_recv.at[b, c, s, 0], me.partner(orders[s % 2][0]),
             )
         yield
-        for s in range(2):
-            strip = pl.ds(256 * s, 256)
+        for s in range(4):
+            strip = pl.ds(128 * s, 128)
             copies[s, 0].wait_recv()
             tb2[c, strip, :] = tb[c, strip, :] + rb1[b, c, strip, :]
-            send(s, 1, tb2.at[c, strip], rb2.at[b, c, strip], orders[s][1])
-        yield
-        for s in range(2):
-            strip = pl.ds(256 * s, 256)
+            send(s, 1, tb2.at[c, strip], rb2.at[b, c, strip], orders[s % 2][1])
+        yield
+        for s in range(4):
+            strip = pl.ds(128 * s, 128)
             copies[s, 1].wait_recv()
             total = tb2[c, strip, :] + rb2[b, c, strip, :]
             if before is not None:
@@ -362,15 +361,15 @@
         mine = lanes_at(256 * me.core + 128 * c, 128)
         pending = []
         own_index = None
-        for q, (l1, l2, l3, l4) in enumerate(LINKS):
+        for q, (l1, l2, l3, l4) in enumerate(STREAMS):
             k1, k2, k3, k4 = me.bit(l1), me.bit(l2), me.bit(l3), me.bit(l4)
-            to_x, to_y, to_z = 2 * k1 + k2, q, me.x
+            to_x, to_y, to_z = 2 * (q % 2) + k1, q // 2, me.x
             index = 2 * k3 + k4
             same = (to_x == me.x) & (to_y == me.y) & (to_z == me.z)
-            own_index = jnp.where(same, index, -1 if own_index is None else own_index)
+            own_index = jnp.where(same, 4 * k2 + index, -1 if own_index is None else own_index)
             copy = remote(
-                h2.at[c, q], share.at[c, index],
-                p_send.at[c, q], p_recv.at[c, index], me.device(x=to_x, y=to_y, z=to_z),
+                h2.at[c, q], share.at[c, k2, index],
+                p_send.at[c, q], p_recv.at[c, k2, index], me.device(x=to_x, y=to_y, z=to_z),
             )
 
             @pl.when(jnp.logical_not(same))
@@ -379,7 +378,7 @@
 
             @pl.when(same)
             def _():
-                share[c, index] = h2[c, q]
+                share[c, k2, index] = h2[c, q]
 
             pending.append((same, copy))
         yield
@@ -389,15 +388,17 @@
             def _():
                 copy.wait_send()
 
-        for index in range(4):
-
-            @pl.when(own_index != index)
-            def _():
-                remote(
-                    h2.at[c, 0], share.at[c, index], p_send.at[c, 0], p_recv.at[c, index], me.sibling()
-                ).wait_recv()
-
-        full[2, :, mine] = (share[c, 0] + share[c, 1]) + (share[c, 2] + share[c, 3])
+        for k2 in range(2):
+            for index in range(4):
+
+                @pl.when(own_index != 4 * k2 + index)
+                def _():
+                    remote(
+                        h2.at[c, 0], share.at[c, k2, index], p_send.at[c, 0], p_recv.at[c, k2, index], me.sibling()
+                    ).wait_recv()
+
+            pieces = [share[c, k2, index] for index in range(4)]
+            full[2, pl.ds(64 * k2, 64), mine] = (pieces[0] + pieces[1]) + (pieces[2] + pieces[3])
         done.add(("z2", c))
 
     half = lanes_at(256 * me.core, 256)
@@ -413,37 +414,41 @@
         copy.wait()
 
     def all_sum(n, target):
-        copies = {}
-
-        def send(s, t, src, dst, link):
-            copies[s, t] = remote(src, dst, a_send.at[n, s, t], a_recv.at[n, s, t], me.partner(link))
-            copies[s, t].start()
-
         def piece(s, k):
             return pl.ds(pl.multiple_of(SUM_START[s] + SUM_HALF[s] * k, 8), SUM_HALF[s])
 
+        small = [pl.ds(0, SUM_HALF[s]) for s in range(6)]
+        keep = [piece(s, me.bit(order[0])) for s, order in enumerate(SUM_LINKS)]
+        away = [piece(s, 1 - me.bit(order[0])) for s, order in enumerate(SUM_LINKS)]
+        copies = {}
         for s, order in enumerate(SUM_LINKS):
-            small = pl.ds(0, SUM_HALF[s])
-            send(s, 0, local.at[n, piece(s, 1 - me.bit(order[0]))], got.at[n, 0, s, small], order[0])
+            for t in range(7):
+                if t == 0:
+                    src, dst = local.at[n, away[s]], got.at[n, 0, s, small[s]]
+                elif t < 6:
+                    src, dst = term.at[n % 2, t - 1, s, small[s]], got.at[n, t, s, small[s]]
+                else:
+                    src = dst = total.at[n, keep[s]]
+                link = order[t % 6]
+                copies[s, t] = remote(src, dst, a_send.at[n, s, t], a_recv.at[n, s, t], me.partner(link))
+        copy = remote(total.at[n], target.at[:, half], x_send.at[n], x_recv.at[n], me.sibling())
+        for s in range(6):
+            copies[s, 0].start()
         yield
         for t in range(1, 6):
-            for s, order in enumerate(SUM_LINKS):
-                small = pl.ds(0, SUM_HALF[s])
+            for s in range(6):
                 copies[s, t - 1].wait_recv()
-                before = local[n, piece(s, me.bit(order[0])), :] if t == 1 else term[n % 2, t - 2, s, small, :]
-                term[n % 2, t - 1, s, small, :] = before + got[n, t - 1, s, small, :]
-                send(s, t, term.at[n % 2, t - 1, s, small], got.at[n, t, s, small], order[t])
+                before = local[n, keep[s], :] if t == 1 else term[n % 2, t - 2, s, small[s], :]
+                term[n % 2, t - 1, s, small[s], :] = before + got[n, t - 1, s, small[s], :]
+                copies[s, t].start()
             yield
-        for s, order in enumerate(SUM_LINKS):
-            small = pl.ds(0, SUM_HALF[s])
+        for s in range(6):
             copies[s, 5].wait_recv()
-            here = piece(s, me.bit(order[0]))
-            total[n, here, :] = term[n % 2, 4, s, small, :] + got[n, 5, s, small, :]
-            send(s, 6, total.at[n, here], total.at[n, here], order[0])
+            total[n, keep[s], :] = term[n % 2, 4, s, small[s], :] + got[n, 5, s, small[s], :]
+            copies[s, 6].start()
         yield
         for s in range(6):
             copies[s, 6].wait_recv()
-        copy = remote(total.at[n], target.at[:, half], x_send.at[n], x_recv.at[n], me.sibling())
         copy.start()
         target[:, half] = total[n]
         for one in copies.values():
@@ -465,8 +470,8 @@
         yield from swap_slab(0)
         local[0] = precise_gram(thirds(full[0]), thirds(full[0, :, half])) / 8192
         yield from all_sum(0, inverse.at[0])
-        for k in range(0, 8, 2):
-            factor_blocks(inverse.at[0], k, k + 2)
+        for k in range(8):
+            factor_block(inverse.at[0], jnp.int32(k))
             yield
         lower_only(inverse.at[0])
         keep_transposed(inverse.at[0])
@@ -482,11 +487,6 @@
         local[1] = precise_gram(thirds(mapped[0]), thirds(mapped[0, :, half])) / 8192
         done.add("filtered")
         yield from all_sum(1, inverse.at[1])
-        for k in range(0, 8, 2):
-            factor_blocks(inverse.at[1], k, k + 2)
-            yield
-        lower_only(inverse.at[1])
-        done.add("second")
 
     def cross_terms():
         yield from needs(("z2", 0), ("z2", 1), "filtered")
@@ -495,11 +495,27 @@
         local[2] = precise_gram(thirds(mapped[0]), thirds(mapped[1, :, half])) / 8192
         yield from all_sum(2, cross)
 
-    live = [chain(0), chain(1), first_factor(), second_factor(), cross_terms()]
-    while live:
+    crossing = cross_terms()
+    live = [chain(0), chain(1), first_factor(), second_factor(), crossing]
+    while len(live) > 1:
         for one in list(live):
             if next(one, "end") == "end":
                 live.remove(one)
+
+    def factor_and_cross(k, carry):
+        factor_block(inverse.at[1], k)
+        for i in range(8):
+
+            @pl.when(k == i)
+            def _():
+                next(crossing, "end")
+
+        return carry
+
+    lax.fori_loop(0, 8, factor_and_cross, 0)
+    for _ in crossing:
+        pass
+    lower_only(inverse.at[1])
 
     keep_transposed(inverse.at[1])
     mine = rows_at(64 * me.core, 64)
@@ -545,14 +561,14 @@
             pltpu.VMEM((2, 2048, 128), F32),
             pltpu.VMEM((2, 512, 256), BF16),
             pltpu.VMEM((2, 2048, 256), BF16),
-            pltpu.VMEM((4, 2, 4, 256, 128), F32),
-            pltpu.VMEM((2, 4, 256, 128), F32),
-            pltpu.VMEM((4, 2, 4, 128, 128), F32),
-            pltpu.VMEM((2, 4, 128, 128), F32),
-            pltpu.VMEM((3, 2, 4, 128, 128), F32),
-            pltpu.VMEM((2, 4, 128, 128), F32),
-            pltpu.VMEM((3, 2, 4, 128, 128), F32),
-            pltpu.VMEM((2, 4, 128, 128), F32),
+            pltpu.VMEM((4, 2, 8, 128, 128), F32),
+            pltpu.VMEM((2, 8, 128, 128), F32),
+            pltpu.VMEM((4, 2, 8, 64, 128), F32),
+            pltpu.VMEM((2, 8, 64, 128), F32),
+            pltpu.VMEM((3, 2, 8, 64, 128), F32),
+            pltpu.VMEM((2, 8, 64, 128), F32),
+            pltpu.VMEM((3, 2, 8, 64, 128), F32),
+            pltpu.VMEM((2, 2, 4, 64, 128), F32),
             pltpu.VMEM((2, 512, 128), F32),
             pltpu.VMEM((3, 2, 512, 128), F32),
             pltpu.VMEM((2, 512, 128), F32),
@@ -567,16 +583,16 @@
             pltpu.VMEM((512, 512), F32),
             pltpu.VMEM((3, 512, 512), BF16),
             pltpu.VMEM((3, 512, 512), BF16),
-            dma((4, 2, 4, 6)),
-            dma((4, 2, 4, 6)),
-            dma((3, 2, 2, 2)),
-            dma((3, 2, 2, 2)),
+            dma((4, 2, 8, 6)),
+            dma((4, 2, 8, 6)),
+            dma((3, 2, 4, 2)),
+            dma((3, 2, 4, 2)),
             dma((8, 2)),
             dma((8, 2)),
             dma,
             dma,
-            dma((2, 4)),
-            dma((2, 4)),
+            dma((2, 8)),
+            dma((2, 2, 4)),
             dma((3,)),
             dma((3,)),
             dma((3, 6, 7)),

time: 247 us -> 239 us (0.968)
  Pallas kernels: 242 us -> 233 us
    pallas_call x1, Pallas kernels: 242 us -> 233 us  [chain_call(): pl.pallas_call(chain_kernel, out_shape=(slab_shape, jax.ShapeDtypeStruct(...]
where the time goes in v1:
time: 239 us; the launch traced here: 238 us
  Pallas kernels  233 us (97%)
  local copies, waits for them, and re-layouts  4.52 us (2%)
    pallas_call x1, Pallas kernels, chain_call(): pl.pallas_call(chain_kernel, out_shape=(slab_shape, jax.ShapeDtypeStruct(...  233 us

profile of v1, /device:TPU:1, one launch (start us, length us, event | category | flops | bytes accessed | tf_op | source)
XLA Modules:
  0.0 238.4 jit_solution(835437687028641190)
XLA Ops:
  0.6 233.2 %shard_map.58 = (f32[64,512]{1,0:T(8,128)}, f32[512,512]{1,0:T(8,128)}, f32[64,512]{1,0:T(8,128)}) custom-call(f32[2]{0:T(128)} %interval.1, f32[1024,512]{1,0:T(8,128)} %matrix.1, f32[64,512]{1,0:T(8,128)} %slab.1), custom_call_target="tpu_custom_call" | custom-call | tf_op jit(solution)/shard_map/pallas_call | solution.py:548
  233.9 0.0 copy-start
  233.9 1.6 copy.9
  235.5 2.3 copy.10
  237.8 0.0 copy-done
  237.8 0.7 copy.11
Async XLA Ops:
  233.9 3.9 %copy-start = (f32[64,512]{1,0:T(8,128)S(1)}, f32[64,512]{1,0:T(8,128)}, u32[]{:S(2)}) copy-start(f32[64,512]{1,0:T(8,128)} %get-tuple-element.8) | copy-start | bytes 393220

commit v2 on v1

--- a/solution.py
+++ b/solution.py
@@ -86,15 +86,20 @@
 def small_factor(tile):
     sub = lax.broadcasted_iota(jnp.int32, (8, 128), 0)
     w = [tile[8 * i : 8 * i + 8, :] for i in range(8)]
+    spread = lambda value, lane: jnp.broadcast_to(value[:, lane : lane + 1], (8, 128))
+    pick = lambda value, row: jnp.broadcast_to(value[row : row + 1, :], (8, 128))
+    ahead = [spread(w[0], c) for c in range(8)]
     for p in range(8):
-        col = {(i, c): jnp.broadcast_to(w[i][:, 8 * p + c : 8 * p + c + 1], (8, 128)) for i in range(p, 8) for c in range(8)}
+        col = {(p, c): ahead[c] for c in range(8)}
+        col.update({(i, c): spread(w[i], 8 * p + c) for i in range(p + 1, 8) for c in range(8)})
+        if p < 7:
+            ahead = [spread(w[p + 1], 8 * p + 8 + c) for c in range(8)]
         for c in range(8):
-            inv = lax.rsqrt(jnp.broadcast_to(col[p, c][c : c + 1, :], (8, 128)))
-            row = jnp.broadcast_to(w[p][c : c + 1, :], (8, 128)) * inv
+            inv = lax.rsqrt(pick(col[p, c], c))
+            row = pick(w[p], c) * inv
             own = col[p, c] * inv
-            below = sub > c
-            w[p] = jnp.where(below, w[p] - own * row, jnp.where(sub == c, row, w[p]))
-            steps = [jnp.broadcast_to(col[p, c][d : d + 1, :], (8, 128)) * inv for d in range(c + 1, 8)]
+            w[p] = jnp.where(sub > c, w[p] - own * row, jnp.where(sub == c, row, w[p]))
+            steps = [pick(col[p, c], d) * inv for d in range(c + 1, 8)]
             for d in range(c + 1, 8):
                 col[p, d] = col[p, d] - own * steps[d - c - 1]
             for i in range(p + 1, 8):
@@ -102,6 +107,8 @@
                 w[i] = w[i] - mult * row
                 for d in range(c + 1, 8):
                     col[i, d] = col[i, d] - mult * steps[d - c - 1]
+                if i == p + 1:
+                    ahead = [ahead[d] - mult * pick(mult, d) for d in range(8)]
     return jnp.concatenate(w, axis=0)
 
 

time: 239 us -> 231 us (0.967)
  Pallas kernels: 233 us -> 226 us
    pallas_call x1, Pallas kernels: 233 us -> 226 us  [chain_call(): pl.pallas_call(chain_kernel, out_shape=(slab_shape, jax.ShapeDtypeStruct(...]
where the time goes in v2:
time: 231 us
  Pallas kernels  226 us (98%)
  local copies, waits for them, and re-layouts  4.52 us (2%)
    pallas_call x1, Pallas kernels, chain_call(): pl.pallas_call(chain_kernel, out_shape=(slab_shape, jax.ShapeDtypeStruct(...  226 us

profile of v2, /device:TPU:1, one launch (start us, length us, event | category | flops | bytes accessed | tf_op | source)
XLA Modules:
  0.0 231.3 jit_solution(10178813022755947916)
XLA Ops:
  0.6 226.1 %shard_map.58 = (f32[64,512]{1,0:T(8,128)}, f32[512,512]{1,0:T(8,128)}, f32[64,512]{1,0:T(8,128)}) custom-call(f32[2]{0:T(128)} %interval.1, f32[1024,512]{1,0:T(8,128)} %matrix.1, f32[64,512]{1,0:T(8,128)} %slab.1), custom_call_target="tpu_custom_call" | custom-call | tf_op jit(solution)/shard_map/pallas_call | solution.py:555
  226.7 0.0 copy-start
  226.8 1.6 copy.9
  228.4 2.3 copy.10
  230.6 0.0 copy-done
  230.6 0.7 copy.11
Async XLA Ops:
  226.7 3.9 %copy-start = (f32[64,512]{1,0:T(8,128)S(1)}, f32[64,512]{1,0:T(8,128)}, u32[]{:S(2)}) copy-start(f32[64,512]{1,0:T(8,128)} %get-tuple-element.8) | copy-start | bytes 393220

commit v3 on v2

--- a/solution.py
+++ b/solution.py
@@ -112,7 +112,7 @@
     return jnp.concatenate(w, axis=0)
 
 
-def factor_block(x, k):
+def factor_block(x, k, below=0):
     here = pl.ds(pl.multiple_of(64 * k, 64), 64)
     pair = pl.ds(pl.multiple_of(128 * (k // 2), 128), 128)
     odd = k % 2
@@ -133,10 +133,12 @@
     lh, lm, ll = thirds(left)
     right = jnp.concatenate([h, m, h, m, l, h], axis=0)
     lefts = jnp.concatenate([lh, lh, lm, lm, lh, ll], axis=0)
-    update = lax.dot_general(lefts, right, (((0,), (0,)), ((), ())), preferred_element_type=F32)
-    r = lax.broadcasted_iota(jnp.int32, (512, 512), 0)
-    c = lax.broadcasted_iota(jnp.int32, (512, 512), 1)
-    x[...] = jnp.where((c // 64 == k) & (r // 64 > k), 0.0, x[...]) - update
+    if below == 512:
+        return
+    update = lax.dot_general(lefts[:, below:], right, (((0,), (0,)), ((), ())), preferred_element_type=F32)
+    r = below + lax.broadcasted_iota(jnp.int32, (512 - below, 512), 0)
+    c = lax.broadcasted_iota(jnp.int32, (512 - below, 512), 1)
+    x[below:, :] = jnp.where((c // 64 == k) & (r // 64 > k), 0.0, x[below:, :]) - update
 
 
 def lower_only(x):
@@ -478,7 +480,7 @@
         local[0] = precise_gram(thirds(full[0]), thirds(full[0, :, half])) / 8192
         yield from all_sum(0, inverse.at[0])
         for k in range(8):
-            factor_block(inverse.at[0], jnp.int32(k))
+            factor_block(inverse.at[0], jnp.int32(k), 128 * ((k + 1) // 2))
             yield
         lower_only(inverse.at[0])
         keep_transposed(inverse.at[0])

time: 231 us -> 230 us (level)
  no operation moved by 1% of the time
where the time goes in v3:
time: 230 us
  Pallas kernels  225 us (98%)
  local copies, waits for them, and re-layouts  4.52 us (2%)
    pallas_call x1, Pallas kernels, chain_call(): pl.pallas_call(chain_kernel, out_shape=(slab_shape, jax.ShapeDtypeStruct(...  225 us

profile of v3, /device:TPU:1, one launch (start us, length us, event | category | flops | bytes accessed | tf_op | source)
XLA Modules:
  0.0 230.3 jit_solution(17374405936502439961)
XLA Ops:
  0.6 225.1 %shard_map.58 = (f32[64,512]{1,0:T(8,128)}, f32[512,512]{1,0:T(8,128)}, f32[64,512]{1,0:T(8,128)}) custom-call(f32[2]{0:T(128)} %interval.1, f32[1024,512]{1,0:T(8,128)} %matrix.1, f32[64,512]{1,0:T(8,128)} %slab.1), custom_call_target="tpu_custom_call" | custom-call | tf_op jit(solution)/shard_map/pallas_call | solution.py:557
  225.8 0.0 copy-start
  225.8 1.6 copy.9
  227.4 2.3 copy.10
  229.6 0.0 copy-done
  229.6 0.7 copy.11
Async XLA Ops:
  225.8 3.9 %copy-start = (f32[64,512]{1,0:T(8,128)S(1)}, f32[64,512]{1,0:T(8,128)}, u32[]{:S(2)}) copy-start(f32[64,512]{1,0:T(8,128)} %get-tuple-element.8) | copy-start | bytes 393220

commit v4 on v3

--- a/solution.py
+++ b/solution.py
@@ -505,7 +505,7 @@
         yield from all_sum(2, cross)
 
     crossing = cross_terms()
-    live = [chain(0), chain(1), first_factor(), second_factor(), crossing]
+    live = [second_factor(), chain(0), chain(1), first_factor(), crossing]
     while len(live) > 1:
         for one in list(live):
             if next(one, "end") == "end":

time: 230 us -> 230 us (level)
  no operation moved by 1% of the time
where the time goes in v4:
time: 230 us
  Pallas kernels  225 us (98%)
  local copies, waits for them, and re-layouts  4.52 us (2%)
    pallas_call x1, Pallas kernels, chain_call(): pl.pallas_call(chain_kernel, out_shape=(slab_shape, jax.ShapeDtypeStruct(...  225 us

profile of v4, /device:TPU:1, one launch (start us, length us, event | category | flops | bytes accessed | tf_op | source)
XLA Modules:
  0.0 230.3 jit_solution(17374405936502439961)
XLA Ops:
  0.6 225.1 %shard_map.58 = (f32[64,512]{1,0:T(8,128)}, f32[512,512]{1,0:T(8,128)}, f32[64,512]{1,0:T(8,128)}) custom-call(f32[2]{0:T(128)} %interval.1, f32[1024,512]{1,0:T(8,128)} %matrix.1, f32[64,512]{1,0:T(8,128)} %slab.1), custom_call_target="tpu_custom_call" | custom-call | tf_op jit(solution)/shard_map/pallas_call | solution.py:557
  225.8 0.0 copy-start
  225.8 1.6 copy.9
  227.4 2.3 copy.10
  229.6 0.0 copy-done
  229.6 0.7 copy.11
Async XLA Ops:
  225.8 3.9 %copy-start = (f32[64,512]{1,0:T(8,128)S(1)}, f32[64,512]{1,0:T(8,128)}, u32[]{:S(2)}) copy-start(f32[64,512]{1,0:T(8,128)} %get-tuple-element.8) | copy-start | bytes 393220
